TPU v7x, 32 devices: a whole 2x2x4 slice. The times are simulated.
32 devices in a mesh: img: 8 (over z, y), sp: 4 (over x, core).
Axes of the slice: x: 2, y: 2, z: 4, core: 2. Of those that a mesh axis runs over, the one named last changes fastest.
Arguments:
- patches: bfloat16 [4096, 1280], P(('img', 'sp')), parts along dimension 0, may hold values from -6 to 6
- pos_ids: int32 [2, 4096], P(None, 'img'), parts along dimension 1, may hold values from 0 to 31, as said below
- norm_gain: float32 [1280], replicated, may hold values from 0.5 to 1.5
- norm_bias: float32 [1280], replicated, may hold values from -3 to 3
- qkv_weight: bfloat16 [1280, 3, 1280], P(None, None, 'sp')
- qkv_bias: float32 [3, 1280], replicated, may hold values from -3 to 3
- proj_weight: bfloat16 [1280, 1280], P('sp'), may hold values from -0.15625 to 0.15625
- proj_bias: float32 [1280], replicated, may hold values from -3 to 3
- merge_gain: float32 [1280], replicated, may hold values from 0.5 to 1.5
- merge_bias: float32 [1280], replicated, may hold values from -3 to 3
- fc1_weight: bfloat16 [5120, 5120], P(None, 'sp'), may hold values from -0.078125 to 0.078125
- fc1_bias: float32 [5120], P('sp'), may hold values from -3 to 3
Outputs:
- vit_out: bfloat16 [4096, 1280], P(('img', 'sp')), parts along dimension 0
- merged_hidden: bfloat16 [1024, 5120], P('img', 'sp'), parts along dimension 0
There are 8 independent parts, one for each index of `img`. A program takes and returns all parts, laid end to end along the dimension named above; an argument that names none is the same for every part. Nothing has to cross between parts.
Inputs may be any that keep to these rules, and one draw needn't show every extreme that they name: pos_ids[0] and pos_ids[1] are the row and column of each patch on a grid of 2 R by 2 C patches, where the grid of 2x2 blocks has R rows and C columns, R C = 128, and one of R and C equals min(8, 128); each aligned run of 4 patches is one 2x2 block in row-major order inside it; every block of the grid appears once, in the order that the argument gives.
All inputs are finite; a program needn't handle non-finite values.
Results may differ from a plain program's by a relative error of at most 0.006.
Values may be sent and summed in bfloat16 or wider, within the bound.
No kernel may reach another device: no remote copies, remote signals or barrier semaphores. Data moves between devices by JAX's collectives and lax.ppermute only.
A program may use at most 64 MiB of HBM per device.

v0:
```python
import jax
import jax.numpy as jnp
from jax import lax
from jax.sharding import PartitionSpec as P

HEADS = 16


def layer_norm(values, gain, bias):
    mean = jnp.mean(values, axis=-1, keepdims=True)
    centered = values - mean
    var = jnp.mean(centered * centered, axis=-1, keepdims=True)
    return centered * lax.rsqrt(var + 1e-06) * gain + bias


def rotate(values, positions, nheads):
    count = values.shape[0]
    hdim = values.shape[1] // nheads
    quarter = hdim // 4
    inv = 1.0 / 10000.0 ** (jnp.arange(quarter, dtype=jnp.float32) * 2.0 / (hdim // 2))
    rows = positions[0].astype(jnp.float32)[:, None] * inv
    cols = positions[1].astype(jnp.float32)[:, None] * inv
    angle = jnp.concatenate([rows, cols, rows, cols], axis=1)
    cosine = jnp.cos(angle)[:, None, :]
    sine = jnp.sin(angle)[:, None, :]
    shaped = values.reshape(count, nheads, hdim)
    half = hdim // 2
    turned = jnp.concatenate([-shaped[..., half:], shaped[..., :half]], axis=-1)
    return (shaped * cosine + turned * sine).reshape(count, nheads * hdim)


def attend(query, keys, value, nheads, hdim):
    count = query.shape[0]
    block = min(512, count)
    qblocks = query.reshape(count // block, block, nheads, hdim)
    kshaped = keys.reshape(count, nheads, hdim)
    vshaped = value.reshape(count, nheads, hdim)
    scale = 1.0 / jnp.sqrt(jnp.float32(hdim))

    def one_block(qpart):
        scores = (
            jnp.einsum("bhd,khd->hbk", qpart, kshaped, preferred_element_type=jnp.float32) * scale
        )
        top = jnp.max(scores, axis=-1, keepdims=True)
        expo = jnp.exp(scores - top)
        weights = (expo / jnp.sum(expo, axis=-1, keepdims=True)).astype(jnp.bfloat16)
        result = jnp.einsum("hbk,khd->bhd", weights, vshaped, preferred_element_type=jnp.float32)
        return result.astype(jnp.bfloat16).reshape(block, nheads * hdim)

    return lax.map(one_block, qblocks).reshape(count, nheads * hdim)


def per_device(
    patches,
    pos_ids,
    norm_gain,
    norm_bias,
    qkv_weight,
    qkv_bias,
    proj_weight,
    proj_bias,
    merge_gain,
    merge_bias,
    fc1_weight,
    fc1_bias,
):
    groups = lax.axis_size("sp")
    where = lax.axis_index("sp")
    prow = patches.shape[0]
    width = patches.shape[1]
    heads_local = HEADS // groups
    hdim = width // HEADS
    local_width = width // groups
    xfloat = patches.astype(jnp.float32)
    normed = layer_norm(xfloat, norm_gain, norm_bias).astype(jnp.bfloat16)
    bias_local = lax.dynamic_slice_in_dim(qkv_bias, where * local_width, local_width, 1)
    qkv = (
        jnp.einsum(
            "pd,dcn->pcn",
            lax.all_gather(normed, "sp", axis=0, tiled=True),
            qkv_weight,
            preferred_element_type=jnp.float32,
        )
        + bias_local[None]
    )
    query = rotate(qkv[:, 0], pos_ids, heads_local).astype(jnp.bfloat16)
    keys = rotate(qkv[:, 1], pos_ids, heads_local).astype(jnp.bfloat16)
    value = qkv[:, 2].astype(jnp.bfloat16)
    spread = jnp.stack([query, keys, value])
    attended = attend(spread[0], spread[1], spread[2], heads_local, hdim)
    returned = lax.all_to_all(attended, "sp", split_axis=0, concat_axis=1, tiled=True)
    projected = jnp.dot(
        returned,
        lax.all_gather(proj_weight, "sp", axis=0, tiled=True),
        preferred_element_type=jnp.float32,
    )
    vit_out = (xfloat + projected + proj_bias).astype(jnp.bfloat16)
    zn = layer_norm(vit_out.astype(jnp.float32), merge_gain, merge_bias).astype(jnp.bfloat16)
    blocks = zn.reshape(prow // 4, 4 * width)
    hidden = (
        jnp.dot(
            lax.all_gather(blocks, "sp", axis=0, tiled=True),
            fc1_weight,
            preferred_element_type=jnp.float32,
        )
        + fc1_bias
    )
    merged_hidden = jax.nn.gelu(hidden, approximate=False).astype(jnp.bfloat16)
    return (vit_out, merged_hidden)


def solution(mesh):
    return jax.shard_map(
        per_device,
        mesh=mesh,
        in_specs=(
            P(("img", "sp"), None),
            P(None, "img"),
            P(),
            P(),
            P(None, None, "sp"),
            P(),
            P("sp", None),
            P(),
            P(),
            P(),
            P(None, "sp"),
            P("sp"),
        ),
        out_specs=(P(("img", "sp"), None), P("img", "sp")),
        check_vma=False,
    )
```

profile of v0, /device:TPU:0, one launch (start us, length us, event | category | flops | bytes accessed | tf_op | source)
XLA Modules:
  0.0 105.2 jit_solution(13298240738997939612)
XLA Ops:
  7.2 1.2 %convert_reduce_fusion = f32[128]{0:T(128)S(1)} fusion(bf16[128,1280]{1,0:T(8,128)(2,1)} %param.12), kind=kLoop, calls=%fused_computation.17 | loop fusion | flops 327552 | bytes 328192 | tf_op jit(solution)/shard_map/reduce_sum | solution.py:10
  8.5 1.2 %fusion.15 = f32[128]{0:T(128)S(1)} fusion(bf16[128,1280]{1,0:T(8,128)(2,1)} %param.12, f32[128]{0:T(128)S(1)} %broadcast_multiply_fusion.3), kind=kLoop, calls=%fused_computation.24 | loop fusion | flops 655232 | bytes 328704 | tf_op jit(solution)/shard_map/reduce_sum | solution.py:12
  9.7 2.0 %fusion.18 = bf16[128,1280]{1,0:T(8,128)(2,1)} fusion(bf16[128,1280]{1,0:T(8,128)(2,1)} %param.12, f32[1280]{0:T(1024)} %param.15, f32[1280]{0:T(1024)} %param.14, f32[128]{0:T(128)S(1)} %add_rsqrt_fusion.1, f32[128]{0:T(128)S(1)} %broadcast_multiply_fusion.3), kind=kLoop, calls=%fused_computation.27 | loop fusion | flops 983040 | bytes 666624 | tf_op jit(solution)/shard_map/convert_element_type | solution.py:75
  11.8 0.7 all-gather.6.cloned.1.call-update
  12.5 0.8 constant_dynamic-slice_fusion
  13.3 0.8 slice_convert_fusion.2
  14.2 0.6 fusion.40
  14.7 18.0 %all-gather.4.cloned.1.call-done = bf16[512,1280]{1,0:T(8,128)(2,1)} async-done(((bf16[128,1280]{1,0:T(8,128)(2,1)}), bf16[512,1280]{1,0:T(8,128)(2,1)}) %all-gather.4.cloned.1.call-update) | async-done | bytes 1310736 | tf_op jit(solution)/shard_map/all_gather | solution.py:80
  32.8 2.8 %convolution_add_fusion.2 = f32[512,3,320]{0,2,1:T(8,128)S(1)} fusion(bf16[1280,3,320]{0,2,1:T(8,128)(2,1)S(1)} %copy-done, bf16[512,1280]{1,0:T(8,128)(2,1)} %all-gather.4.cloned.1.call-done, f32[3,320]{1,0:T(4,128)S(1)} %constant_dynamic-slice_fusion), kind=kOutput, calls=%fused_computation.11 | convolution fusion | flops 1258782720 | bytes 5738240 | tf_op jit(solution)/shard_map/pd,dcn->pcn/dot_general | solution.py:78
  35.5 0.8 slice.51
  36.3 0.1 fusion.42
  36.4 0.1 slice_negate_fusion
  36.6 0.4 fusion.29
  37.0 3.4 %fusion.43 = (f32[4,512]{1,0:T(4,128)S(1)}, f32[4,512,512]{1,2,0:T(8,128)}) fusion(bf16[512,4,80]{0,2,1:T(8,128)(2,1)S(1)} %get-tuple-element.24, bf16[512,4,80]{0,2,1:T(8,128)(2,1)S(1)} %get-tuple-element.23), kind=kOutput, calls=%fused_computation.75 | convolution fusion | flops 170918400 | bytes 4857856 | tf_op jit(solution)/shard_map/while/body/eval_jaxpr/sub | solution.py:45
  40.4 3.1 %fusion.10 = bf16[512,4,80]{0,2,1:T(8,128)(2,1)S(1)} fusion(bf16[512,4,80]{0,2,1:T(8,128)(2,1)S(1)} %bitcast.30, f32[4,512,512]{1,2,0:T(8,128)} %get-tuple-element.32, f32[4,512]{1,0:T(4,128)S(1)} %get-tuple-element.31), kind=kOutput, calls=%fused_computation.14 | convolution fusion | flops 170033152 | bytes 4857856 | tf_op jit(solution)/shard_map/while/body/eval_jaxpr/hbk,khd->bhd/dot_general | solution.py:47
  43.5 0.1 all_to_all.14
  43.6 13.0 %all_to_all.19 = bf16[4,128,320]{1,2,0:T(8,128)(2,1)S(1)} all-to-all(bf16[4,128,320]{1,2,0:T(8,128)(2,1)S(1)} %copy.16), channel_id=1, replica_groups=mesh['img'=8,'sp'=4] {'sp'}, dimensions={0} | all-to-all | bytes 655360 | tf_op jit(solution)/shard_map/all_to_all | solution.py:91
  56.6 10.5 %all-gather.6.cloned.1.call-done = bf16[1280,1280]{1,0:T(8,128)(2,1)} async-done(((bf16[320,1280]{1,0:T(8,128)(2,1)}), bf16[1280,1280]{1,0:T(8,128)(2,1)}) %all-gather.6.cloned.1.call-update) | async-done | bytes 3276816 | tf_op jit(solution)/shard_map/all_gather | solution.py:94
  67.1 2.7 %convert_reduce_fusion.1 = (f32[128]{0:T(128)S(1)}, bf16[128,1280]{1,0:T(8,128)(2,1)S(1)}) fusion(f32[1280]{0:T(1024)S(1)} %copy-done.4, bf16[128,1280]{0,1:T(8,128)(2,1)S(1)} %bitcast.29, bf16[1280,1280]{1,0:T(8,128)(2,1)} %all-gather.6.cloned.1.call-done, bf16[128,1280]{1,0:T(8,128)(2,1)S(1)} %copy-done.1), kind=kOutput, calls=%fused_computation.19 | convolution fusion | flops 420413312 | bytes 4265472 | tf_op jit(solution)/shard_map/dot_general | solution.py:92
  69.8 0.2 fusion.19
  70.1 0.3 fusion.22
  70.4 0.9 reshape.180
  71.3 18.3 %all-gather.8.cloned.1.call-done = bf16[128,5120]{1,0:T(8,128)(2,1)} async-done(((bf16[32,5120]{1,0:T(8,128)(2,1)}), bf16[128,5120]{1,0:T(8,128)(2,1)}) %all-gather.8.cloned.1.call-update) | async-done | bytes 1310736 | tf_op jit(solution)/shard_map/all_gather | solution.py:102
  89.6 9.1 %fusion.25 = bf16[128,1280]{1,0:T(8,128)(2,1)} fusion(bf16[128,5120]{1,0:T(8,128)(2,1)} %all-gather.8.cloned.1.call-done, bf16[5120,1280]{1,0:T(8,128)(2,1)} %param.22, f32[1280]{0:T(1024)S(1)} %copy-done.7), kind=kOutput, calls=%fused_computation.34 | convolution fusion | flops 1688535040 | bytes 14750720 | tf_op jit(solution)/shard_map/dot_general | solution.py:101
  (28 shorter events, 0.4 us)
Async XLA Ops:
  7.2 25.6 %copy-start = (bf16[1280,3,320]{0,2,1:T(8,128)(2,1)S(1)}, bf16[1280,3,320]{0,2,1:T(8,128)(2,1)}, u32[]{:S(2)}) copy-start(bf16[1280,3,320]{0,2,1:T(8,128)(2,1)} %param.16) | copy-start | bytes 7372804
  7.2 25.6 %all-gather.4.cloned.1.call-start = ((), (), s32[]{:S(2)}) async-start(), calls=%async_computation.1 | async-start | bytes 1638400 | tf_op jit(solution)/shard_map/all_gather | solution.py:80
  11.7 55.4 %all-gather.6.cloned.1.call-start = ((), (), s32[]{:S(2)}) async-start(), calls=%async_computation.2 | async-start | bytes 4096000 | tf_op jit(solution)/shard_map/all_gather | solution.py:94
  12.5 77.2 %all-gather.8.cloned.1.call-start = ((), (), s32[]{:S(2)}) async-start(), calls=%async_computation.3 | async-start | bytes 1638400 | tf_op jit(solution)/shard_map/all_gather | solution.py:102
  36.9 3.5 %copy-start.3 = (bf16[512,1,320]{0,2,1:T(8,128)(2,1)S(1)}, bf16[512,1,320]{0,2,1:T(8,128)(2,1)}, u32[]{:S(2)}) copy-start(bf16[512,1,320]{0,2,1:T(8,128)(2,1)} %slice.51) | copy-start | bytes 983044
  40.4 26.7 %copy-start.1 = (bf16[128,1280]{1,0:T(8,128)(2,1)S(1)}, bf16[128,1280]{1,0:T(8,128)(2,1)}, u32[]{:S(2)}) copy-start(bf16[128,1280]{1,0:T(8,128)(2,1)} %param.12) | copy-start | bytes 983044
  40.4 26.7 %copy-start.4 = (f32[1280]{0:T(1024)S(1)}, f32[1280]{0:T(1024)}, u32[]{:S(2)}) copy-start(f32[1280]{0:T(1024)} %param.19) | copy-start | bytes 15364
  43.5 26.6 %copy-start.5 = (f32[1280]{0:T(1024)S(1)}, f32[1280]{0:T(1024)}, u32[]{:S(2)}) copy-start(f32[1280]{0:T(1024)} %param.21) | copy-start | bytes 15364
  43.5 26.6 %copy-start.6 = (f32[1280]{0:T(1024)S(1)}, f32[1280]{0:T(1024)}, u32[]{:S(2)}) copy-start(f32[1280]{0:T(1024)} %param.20) | copy-start | bytes 15364
  56.6 33.0 %copy-start.7 = (f32[1280]{0:T(1024)S(1)}, f32[1280]{0:T(1024)}, u32[]{:S(2)}) copy-start(f32[1280]{0:T(1024)} %param.23) | copy-start | bytes 15364
  69.8 28.9 %copy-start.2 = (bf16[128,1280]{1,0:T(8,128)(2,1)}, bf16[128,1280]{1,0:T(8,128)(2,1)S(1)}, u32[]{:S(2)}) copy-start(bf16[128,1280]{1,0:T(8,128)(2,1)S(1)} %get-tuple-element.34) | copy-start | bytes 983044
Sparse Core Ops, SparseCore 0:
  11.8 20.8 all-gather.3
  34.3 32.7 all-gather.5
  71.4 18.1 all-gather.7
where the time goes:
time: 106 us; the launch traced here: 105 us
  waiting for transfers between devices  47.5 us (45%)
  matrix products  21 us (20%)
  between operations  13.9 us (13%)
  blocking collectives  13 us (12%)
  other arithmetic  6.95 us (7%)
  local copies, waits for them, and re-layouts  2.74 us (3%)
    all_gather x1, waiting for transfers between devices, per_device(): lax.all_gather(blocks, 'sp', axis=0, tiled=True)  18.3 us
    all_gather x1, waiting for transfers between devices, per_device(): lax.all_gather(normed, 'sp', axis=0, tiled=True)  18 us
    all_to_all x1, blocking collectives, per_device(): lax.all_to_all(attended, 'sp', split_axis=0, concat_axis=1, tiled=True)  13 us
    all_gather x1, waiting for transfers between devices, per_device(): lax.all_gather(proj_weight, 'sp', axis=0, tiled=True)  10.5 us
    dot_general x1, matrix products, per_device(): jnp.dot(lax.all_gather(blocks, 'sp', axis=0, tiled=True), fc1_weight, pre...  9.06 us
    sub x1, matrix products, one_block(): expo = jnp.exp(scores - top)  3.44 us
    dot_general x1, matrix products, one_block(): jnp.einsum('hbk,khd->bhd', weights, vshaped, preferred_element_type=jnp.f...  3.07 us
    dot_general x1, matrix products, per_device(): jnp.einsum('pd,dcn->pcn', lax.all_gather(normed, 'sp', axis=0, tiled=True...  2.77 us
  transfers between devices with their start and end apart: 3, of which 3 were waited for; matrix products, arithmetic and copies ran while one was open for 12% of the time, Pallas kernels for 0%

commit v1 on v0

--- a/solution.py
+++ b/solution.py
@@ -4,6 +4,20 @@
 from jax.sharding import PartitionSpec as P
 
 HEADS = 16
+
+
+def on_each_block(x, axis, dim, make, out_dim):
+    ways, here, step = (lax.axis_size(axis), lax.axis_index(axis), x.shape[dim])
+    earlier, later = ([], [])
+    going_up = going_down = x
+    for far in range(ways // 2 + 1):
+        earlier.append(make(going_up, (here - far) % ways * step))
+        if 0 < far < ways - ways // 2:
+            later.append(make(going_down, (here + far) % ways * step))
+        going_up = lax.ppermute(going_up, axis, [(d, (d + 1) % ways) for d in range(ways)])
+        going_down = lax.ppermute(going_down, axis, [(d, (d - 1) % ways) for d in range(ways)])
+    line = jnp.concatenate([*earlier[::-1], *later], axis=out_dim)
+    return jnp.roll(line, (here - ways // 2) * earlier[0].shape[out_dim], axis=out_dim)
 
 
 def layer_norm(values, gain, bias):
@@ -75,11 +89,14 @@
     normed = layer_norm(xfloat, norm_gain, norm_bias).astype(jnp.bfloat16)
     bias_local = lax.dynamic_slice_in_dim(qkv_bias, where * local_width, local_width, 1)
     qkv = (
-        jnp.einsum(
-            "pd,dcn->pcn",
-            lax.all_gather(normed, "sp", axis=0, tiled=True),
-            qkv_weight,
-            preferred_element_type=jnp.float32,
+        on_each_block(
+            normed,
+            "sp",
+            0,
+            lambda shard, at: jnp.einsum(
+                "pd,dcn->pcn", shard, qkv_weight, preferred_element_type=jnp.float32
+            ),
+            0,
         )
         + bias_local[None]
     )

time: 106 us -> 96.1 us (0.907)
  waiting for transfers between devices: 47.5 us -> 30.5 us
  starting transfers between devices: 0.12 us -> 6.77 us
  blocking collectives: 13 us -> 14.6 us
    all_gather x1 -> x0, waiting for transfers between devices: 18 us -> none  [per_device(): lax.all_gather(normed, 'sp', axis=0, tiled=True)]
    ppermute x0 -> x3, waiting for transfers between devices: none -> 12.6 us  [the longest x2 12.6 us: on_each_block(): lax.ppermute(going_up, axis, [(d, (d + 1) % ways) for d in range(ways)])]
    all_gather x1, waiting for transfers between devices: 10.5 us -> 0.01 us  [per_device(): lax.all_gather(proj_weight, 'sp', axis=0, tiled=True)]
    ppermute x0 -> x3, starting transfers between devices: none -> 6.69 us  [the longest x2 4.71 us: on_each_block(): lax.ppermute(going_up, axis, [(d, (d + 1) % ways) for d in range(ways)])]
    all_to_all x1, blocking collectives: 13 us -> 14.6 us  [per_device(): lax.all_to_all(attended, 'sp', split_axis=0, concat_axis=1, tiled=True)]
    all_gather x1, waiting for transfers between devices: 18.3 us -> 17.2 us  [per_device(): lax.all_gather(blocks, 'sp', axis=0, tiled=True)]
    dot_general x1 -> x4, matrix products: 2.77 us -> 3.17 us  [per_device(): jnp.einsum('pd,dcn->pcn', shard, qkv_weight, preferred_element_type=jnp.f...]
  transfers between devices with their start and end apart: 3 -> 5, of which waited for: 3 -> 3; matrix products, arithmetic and copies ran while one was open for 12% -> 17% of each run, Pallas kernels for 0% -> 0%
where the time goes in v1:
time: 96.1 us; the launch traced here: 95.7 us
  waiting for transfers between devices  30.5 us (32%)
  matrix products  21.1 us (22%)
  blocking collectives  14.6 us (15%)
  between operations  14.2 us (15%)
  starting transfers between devices  6.77 us (7%)
  other arithmetic  6.27 us (7%)
  local copies, waits for them, and re-layouts  2.25 us (2%)
    all_gather x1, waiting for transfers between devices, per_device(): lax.all_gather(blocks, 'sp', axis=0, tiled=True)  17.2 us
    all_to_all x1, blocking collectives, per_device(): lax.all_to_all(attended, 'sp', split_axis=0, concat_axis=1, tiled=True)  14.6 us
    ppermute x2, waiting for transfers between devices, on_each_block(): lax.ppermute(going_up, axis, [(d, (d + 1) % ways) for d in range(ways)])  12.6 us
    dot_general x1, matrix products, per_device(): jnp.dot(lax.all_gather(blocks, 'sp', axis=0, tiled=True), fc1_weight, pre...  9.06 us
    ppermute x2, starting transfers between devices, on_each_block(): lax.ppermute(going_up, axis, [(d, (d + 1) % ways) for d in range(ways)])  4.71 us
    sub x1, matrix products, one_block(): expo = jnp.exp(scores - top)  3.45 us
    dot_general x4, matrix products, per_device(): jnp.einsum('pd,dcn->pcn', shard, qkv_weight, preferred_element_type=jnp.f...  3.17 us
    dot_general x1, matrix products, one_block(): jnp.einsum('hbk,khd->bhd', weights, vshaped, preferred_element_type=jnp.f...  2.77 us
  transfers between devices with their start and end apart: 5, of which 3 were waited for; matrix products, arithmetic and copies ran while one was open for 17% of the time, Pallas kernels for 0%

profile of v1, /device:TPU:0, one launch (start us, length us, event | category | flops | bytes accessed | tf_op | source)
XLA Modules:
  0.0 95.7 jit_solution(3878398327765603300)
XLA Ops:
  7.2 0.7 all-gather.3.cloned.1.call-update
  8.0 1.1 %convert_reduce_fusion = f32[128]{0:T(128)S(1)} fusion(bf16[128,1280]{1,0:T(8,128)(2,1)} %param.12), kind=kLoop, calls=%fused_computation.16 | loop fusion | flops 327552 | bytes 328192 | tf_op jit(solution)/shard_map/reduce_sum | solution.py:24
  9.1 1.2 %fusion.14 = f32[128]{0:T(128)S(1)} fusion(bf16[128,1280]{1,0:T(8,128)(2,1)} %param.12, f32[128]{0:T(128)S(1)} %broadcast_multiply_fusion.3), kind=kLoop, calls=%fused_computation.23 | loop fusion | flops 655232 | bytes 328704 | tf_op jit(solution)/shard_map/reduce_sum | solution.py:26
  10.3 1.3 %fusion.17 = bf16[128,1280]{1,0:T(8,128)(2,1)S(1)} fusion(bf16[128,1280]{1,0:T(8,128)(2,1)} %param.12, f32[1280]{0:T(1024)} %param.15, f32[1280]{0:T(1024)} %param.14, f32[128]{0:T(128)S(1)} %add_rsqrt_fusion.1, f32[128]{0:T(128)S(1)} %broadcast_multiply_fusion.3), kind=kLoop, calls=%fused_computation.26 | loop fusion | flops 983040 | bytes 666624 | tf_op jit(solution)/shard_map/convert_element_type | solution.py:89
  11.6 0.5 collective-permute-start
  12.1 2.0 %collective-permute-start.2 = (bf16[128,1280]{1,0:T(8,128)(2,1)S(1)}, bf16[128,1280]{1,0:T(8,128)(2,1)S(1)}, u32[]{:S(2)}, u32[]{:S(2)}) collective-permute-start(bf16[128,1280]{1,0:T(8,128)(2,1)S(1)} %fusion.17), channel_id=1, source_target_pairs={{0,3},{1,0},{2,1},{3,2},{4,7},{5,4},{6,5},{7,6},{8,11},{9,8},{10,9... | collective-permute-start | bytes 983048 | tf_op jit(solution)/shard_map/ppermute | solution.py:18
  14.1 0.8 constant_dynamic-slice_fusion
  14.9 0.8 slice_convert_fusion.2
  15.6 4.1 %collective-permute-done = bf16[128,1280]{1,0:T(8,128)(2,1)S(1)} collective-permute-done((bf16[128,1280]{1,0:T(8,128)(2,1)S(1)}, bf16[128,1280]{1,0:T(8,128)(2,1)S(1)}, u32[]{:S(2)}, u32[]{:S(2)}) %collective-permute-start) | collective-permute-done | bytes 327712 | tf_op jit(solution)/shard_map/ppermute | solution.py:17
  19.7 4.2 %collective-permute-start.1 = (bf16[128,1280]{1,0:T(8,128)(2,1)S(1)}, bf16[128,1280]{1,0:T(8,128)(2,1)S(1)}, u32[]{:S(2)}, u32[]{:S(2)}) collective-permute-start(bf16[128,1280]{1,0:T(8,128)(2,1)S(1)} %collective-permute-done), channel_id=1, source_target_pairs={{0,1},{1,2},{2,3},{3,0},{4,5},{5,6},{6,7},{7,4},{8,9},{9,10},{10,1... | collective-permute-start | bytes 983048 | tf_op jit(solution)/shard_map/ppermute | solution.py:17
  23.9 0.6 fusion.47
  24.5 8.5 %collective-permute-done.1 = bf16[128,1280]{1,0:T(8,128)(2,1)S(1)} collective-permute-done((bf16[128,1280]{1,0:T(8,128)(2,1)S(1)}, bf16[128,1280]{1,0:T(8,128)(2,1)S(1)}, u32[]{:S(2)}, u32[]{:S(2)}) %collective-permute-start.1) | collective-permute-done | bytes 327712 | tf_op jit(solution)/shard_map/ppermute | solution.py:17
  33.0 0.8 constant_dynamic-update-slice_fusion.7
  33.8 0.8 constant_dynamic-update-slice_fusion.6
  34.6 0.8 constant_dynamic-update-slice_fusion.5
  35.4 0.8 constant_dynamic-update-slice_fusion.4
  37.0 0.4 fusion.28
  37.4 3.4 %fusion.50 = (f32[4,512]{1,0:T(4,128)S(1)}, f32[4,512,512]{1,2,0:T(8,128)}) fusion(bf16[512,4,80]{0,2,1:T(8,128)(2,1)S(1)} %get-tuple-element.24, bf16[512,4,80]{0,2,1:T(8,128)(2,1)S(1)} %get-tuple-element.23), kind=kOutput, calls=%fused_computation.90 | convolution fusion | flops 170918400 | bytes 4857856 | tf_op jit(solution)/shard_map/while/body/eval_jaxpr/sub | solution.py:59
  40.9 2.8 %fusion.9 = bf16[512,4,80]{0,2,1:T(8,128)(2,1)S(1)} fusion(bf16[512,4,80]{0,2,1:T(8,128)(2,1)S(1)} %bitcast.50, f32[4,512,512]{1,2,0:T(8,128)} %get-tuple-element.40, f32[4,512]{1,0:T(4,128)S(1)} %get-tuple-element.39), kind=kOutput, calls=%fused_computation.13 | convolution fusion | flops 170033152 | bytes 4857856 | tf_op jit(solution)/shard_map/while/body/eval_jaxpr/hbk,khd->bhd/dot_general | solution.py:61
  43.8 14.6 %all_to_all.19 = bf16[4,128,320]{1,2,0:T(8,128)(2,1)S(1)} all-to-all(bf16[4,128,320]{1,2,0:T(8,128)(2,1)S(1)} %copy.16), channel_id=1, replica_groups=mesh['img'=8,'sp'=4] {'sp'}, dimensions={0} | all-to-all | bytes 655360 | tf_op jit(solution)/shard_map/all_to_all | solution.py:108
  58.4 2.7 %convert_reduce_fusion.1 = (f32[128]{0:T(128)S(1)}, bf16[128,1280]{1,0:T(8,128)(2,1)S(1)}) fusion(f32[1280]{0:T(1024)S(1)} %copy-done.3, bf16[128,1280]{0,1:T(8,128)(2,1)S(1)} %bitcast.49, bf16[1280,1280]{1,0:T(8,128)(2,1)} %all-gather.3.cloned.1.call-done, bf16[128,1280]{1,0:T(8,128)(2,1)S(1)} %copy-done.1), kind=kOutput, calls=%fused_computation.18 | convolution fusion | flops 420413312 | bytes 4265472 | tf_op jit(solution)/shard_map/dot_general | solution.py:109
  61.6 0.9 reshape.180
  62.6 17.2 %all-gather.5.cloned.1.call-done = bf16[128,5120]{1,0:T(8,128)(2,1)} async-done(((bf16[32,5120]{1,0:T(8,128)(2,1)}), bf16[128,5120]{1,0:T(8,128)(2,1)}) %all-gather.5.cloned.1.call-update) | async-done | bytes 1310736 | tf_op jit(solution)/shard_map/all_gather | solution.py:119
  79.8 9.1 %fusion.24 = bf16[128,1280]{1,0:T(8,128)(2,1)} fusion(bf16[128,5120]{1,0:T(8,128)(2,1)} %all-gather.5.cloned.1.call-done, bf16[5120,1280]{1,0:T(8,128)(2,1)} %param.22, f32[1280]{0:T(1024)S(1)} %copy-done.6), kind=kOutput, calls=%fused_computation.33 | convolution fusion | flops 1688535040 | bytes 14750720 | tf_op jit(solution)/shard_map/dot_general | solution.py:118
  (37 shorter events, 1.6 us)
Async XLA Ops:
  7.2 25.9 %copy-start = (bf16[1280,3,320]{0,2,1:T(8,128)(2,1)S(1)}, bf16[1280,3,320]{0,2,1:T(8,128)(2,1)}, u32[]{:S(2)}) copy-start(bf16[1280,3,320]{0,2,1:T(8,128)(2,1)} %param.16) | copy-start | bytes 7372804
  7.2 51.2 %all-gather.3.cloned.1.call-start = ((), (), s32[]{:S(2)}) async-start(), calls=%async_computation.1 | async-start | bytes 4096000 | tf_op jit(solution)/shard_map/all_gather | solution.py:111
  7.9 71.9 %all-gather.5.cloned.1.call-start = ((), (), s32[]{:S(2)}) async-start(), calls=%async_computation.2 | async-start | bytes 1638400 | tf_op jit(solution)/shard_map/all_gather | solution.py:119
  11.6 8.1 %collective-permute-start = (bf16[128,1280]{1,0:T(8,128)(2,1)S(1)}, bf16[128,1280]{1,0:T(8,128)(2,1)S(1)}, u32[]{:S(2)}, u32[]{:S(2)}) collective-permute-start(bf16[128,1280]{1,0:T(8,128)(2,1)S(1)} %fusion.17), channel_id=1, source_target_pairs={{0,1},{1,2},{2,3},{3,0},{4,5},{5,6},{6,7},{7,4},{8,9},{9,10},{10,1... | collective-permute-start | bytes 983048 | tf_op jit(solution)/shard_map/ppermute | solution.py:17
  12.1 23.3 %collective-permute-start.2 = (bf16[128,1280]{1,0:T(8,128)(2,1)S(1)}, bf16[128,1280]{1,0:T(8,128)(2,1)S(1)}, u32[]{:S(2)}, u32[]{:S(2)}) collective-permute-start(bf16[128,1280]{1,0:T(8,128)(2,1)S(1)} %fusion.17), channel_id=1, source_target_pairs={{0,3},{1,0},{2,1},{3,2},{4,7},{5,4},{6,5},{7,6},{8,11},{9,8},{10,9... | collective-permute-start | bytes 983048 | tf_op jit(solution)/shard_map/ppermute | solution.py:18
  19.7 13.3 %collective-permute-start.1 = (bf16[128,1280]{1,0:T(8,128)(2,1)S(1)}, bf16[128,1280]{1,0:T(8,128)(2,1)S(1)}, u32[]{:S(2)}, u32[]{:S(2)}) collective-permute-start(bf16[128,1280]{1,0:T(8,128)(2,1)S(1)} %collective-permute-done), channel_id=1, source_target_pairs={{0,1},{1,2},{2,3},{3,0},{4,5},{5,6},{6,7},{7,4},{8,9},{9,10},{10,1... | collective-permute-start | bytes 983048 | tf_op jit(solution)/shard_map/ppermute | solution.py:17
  40.9 17.5 %copy-start.1 = (bf16[128,1280]{1,0:T(8,128)(2,1)S(1)}, bf16[128,1280]{1,0:T(8,128)(2,1)}, u32[]{:S(2)}) copy-start(bf16[128,1280]{1,0:T(8,128)(2,1)} %param.12) | copy-start | bytes 983044
  40.9 17.5 %copy-start.3 = (f32[1280]{0:T(1024)S(1)}, f32[1280]{0:T(1024)}, u32[]{:S(2)}) copy-start(f32[1280]{0:T(1024)} %param.19) | copy-start | bytes 15364
  43.6 17.7 %copy-start.4 = (f32[1280]{0:T(1024)S(1)}, f32[1280]{0:T(1024)}, u32[]{:S(2)}) copy-start(f32[1280]{0:T(1024)} %param.21) | copy-start | bytes 15364
  43.6 17.7 %copy-start.5 = (f32[1280]{0:T(1024)S(1)}, f32[1280]{0:T(1024)}, u32[]{:S(2)}) copy-start(f32[1280]{0:T(1024)} %param.20) | copy-start | bytes 15364
  43.7 36.1 %copy-start.6 = (f32[1280]{0:T(1024)S(1)}, f32[1280]{0:T(1024)}, u32[]{:S(2)}) copy-start(f32[1280]{0:T(1024)} %param.23) | copy-start | bytes 15364
  61.1 27.8 %copy-start.2 = (bf16[128,1280]{1,0:T(8,128)(2,1)}, bf16[128,1280]{1,0:T(8,128)(2,1)S(1)}, u32[]{:S(2)}) copy-start(bf16[128,1280]{1,0:T(8,128)(2,1)S(1)} %get-tuple-element.42) | copy-start | bytes 983044
Sparse Core Ops, SparseCore 0:
  9.5 35.4 all-gather.2
  62.7 17.0 all-gather.4
